TPU v7x, 32 devices: a whole 2x2x4 slice. The times are simulated.
32 devices in a mesh: member: 2 (over x), band: 16 (over z, y, core).
Axes of the slice: x: 2, y: 2, z: 4, core: 2. Of those that a mesh axis runs over, the one named last changes fastest.
Arguments:
- grid_in: bfloat16 [32, 274, 5248], P(('member', 'band')), parts along dimension 0, may hold values from -6 to 6
- legendre: bfloat16 [16, 2, 640, 8], P('band'), may hold values from -2 to 2
- gauss_weight: float32 [8], replicated, may hold values from 0.2 to 2
- vertical_modes: float32 [137, 137], replicated
- coupling: float32 [137, 137], replicated, may hold values from -0.5 to 0.5
- mode_rates: float32 [137], replicated, may hold values from 0.1 to 10
- loop_length: int32 [16], replicated, may hold values from 20 to 5136, as said below
- lat_order: int32 [16], replicated, may hold values from 0 to 15, each once
- wave_number: int32 [16], replicated, may hold values from 0 to 1279, as said below
Outputs:
- grid_out: bfloat16 [32, 274, 5248], P(('member', 'band')), parts along dimension 0
There are 2 independent parts, one for each index of `member`. A program takes and returns all parts, laid end to end along the dimension named above; an argument that names none is the same for every part. Nothing has to cross between parts.
Inputs may be any that keep to these rules, and one draw needn't show every extreme that they name: loop_length[t] = 20 + 4 k with k not falling from the poles toward the equator, equal for latitudes t and 15 - t; the equatorial loops have 5248 - 112 points. Row i of grid_in and grid_out holds latitude lat_order[i]. `wave_number`: distinct values.
All inputs are finite; a program needn't handle non-finite values.
Results may differ from a plain program's by a relative error of at most 0.013.
Values may be sent and summed in bfloat16 or wider, within the bound.
A program may use at most 64 MiB of HBM per device.

v0:
```python
import math
import jax
import jax.numpy as jnp
from jax import lax
from jax.sharding import PartitionSpec as P

TRUNC = 1279
implicit_step = 0.5
highest = lax.Precision.HIGHEST


def loop_tables(length, wave_list, block_count):
    offsets = jnp.arange(128, dtype=jnp.int32)
    inner_turn = offsets[:, None] * wave_list[None, :] % length
    angles = inner_turn.astype(jnp.float32) * (2.0 * math.pi) / length.astype(jnp.float32)
    inner_table = jnp.concatenate([jnp.cos(angles), jnp.sin(angles)], axis=1).astype(jnp.bfloat16)
    block_index = jnp.arange(block_count, dtype=jnp.int32)
    outer_turn = block_index[:, None] * 128 * wave_list[None, :] % length
    phases = outer_turn.astype(jnp.float32) * (2.0 * math.pi) / length.astype(jnp.float32)
    return (inner_table, jnp.cos(phases), jnp.sin(phases))


def forward_loop(one_loop, length, wave_list):
    field_count, loop_width = one_loop.shape
    block_count = loop_width // 128
    wave_count = wave_list.shape[0]
    inner_table, cos_turn, sin_turn = loop_tables(length, wave_list, block_count)
    inside = jnp.arange(loop_width, dtype=jnp.int32) < length
    masked = jnp.where(inside[None, :], one_loop, jnp.zeros((), one_loop.dtype))
    products = jnp.dot(
        masked.reshape(field_count * block_count, 128),
        inner_table,
        preferred_element_type=jnp.float32,
    )
    products = products.reshape(field_count, block_count, 2, wave_count)
    real_part = jnp.sum(cos_turn * products[:, :, 0] - sin_turn * products[:, :, 1], axis=1)
    imag_part = -jnp.sum(sin_turn * products[:, :, 0] + cos_turn * products[:, :, 1], axis=1)
    inverse_len = 1.0 / length.astype(jnp.float32)
    together = jnp.concatenate([real_part, imag_part], axis=0) * inverse_len
    resolved = 2 * wave_list < length
    together = jnp.where(resolved[None, :], together, 0.0)
    return together.T.astype(jnp.bfloat16)


def inverse_loop(fourier, length, wave_list, loop_width):
    block_count = loop_width // 128
    wave_count = wave_list.shape[0]
    field_count = fourier.shape[1] // 2
    inner_table, cos_turn, sin_turn = loop_tables(length, wave_list, block_count)
    doubling = jnp.where(wave_list == 0, 1.0, 2.0).astype(jnp.float32)
    real_part = fourier[:, :field_count].astype(jnp.float32).T * doubling
    imag_part = fourier[:, field_count:].astype(jnp.float32).T * doubling
    cosine_part = real_part[:, None, :] * cos_turn[None] - imag_part[:, None, :] * sin_turn[None]
    sine_part = -(real_part[:, None, :] * sin_turn[None] + imag_part[:, None, :] * cos_turn[None])
    combined = jnp.concatenate([cosine_part, sine_part], axis=2).astype(jnp.bfloat16)
    points = lax.dot_general(
        combined.reshape(field_count * block_count, 2 * wave_count),
        inner_table,
        (((1,), (1,)), ((), ())),
        preferred_element_type=jnp.float32,
    )
    points = points.reshape(field_count, loop_width)
    inside = jnp.arange(loop_width, dtype=jnp.int32) < length
    return jnp.where(inside[None, :], points, 0.0).astype(jnp.bfloat16)


def semi_implicit(spectral, wave_values, vertical_modes, coupling, mode_rates):
    half_rows = spectral.shape[-2]
    level_count = vertical_modes.shape[0]
    parity = jnp.arange(2, dtype=jnp.int32)
    row_index = jnp.arange(half_rows, dtype=jnp.int32)
    degree = wave_values[..., None, None] + parity[:, None] + 2 * row_index[None, :]
    kept_rows = degree <= TRUNC
    spectral = jnp.where(kept_rows[..., None], spectral, 0.0)
    damping = (degree * (degree + 1)).astype(jnp.float32) / float(TRUNC * (TRUNC + 1))
    reshaped = spectral.reshape(spectral.shape[:-1] + (2, 2, level_count))
    divergence = reshaped[..., 0, :]
    pressure = reshaped[..., 1, :]
    factor_e = damping[..., None, None]
    right_side = divergence - implicit_step * factor_e * jnp.einsum(
        "...l,kl->...k", pressure, coupling, precision=highest
    )
    in_modes = jnp.einsum("...l,lk->...k", right_side, vertical_modes, precision=highest)
    in_modes = in_modes / (1.0 + implicit_step * factor_e * mode_rates)
    new_div = jnp.einsum("...k,lk->...l", in_modes, vertical_modes, precision=highest)
    new_press = pressure - implicit_step * jnp.einsum(
        "...l,kl->...k", new_div, coupling, precision=highest
    )
    updated = jnp.stack([new_div, new_press], axis=-2)
    return updated.reshape(spectral.shape).astype(jnp.bfloat16)


def per_device(
    grid_in,
    legendre,
    gauss_weight,
    vertical_modes,
    coupling,
    mode_rates,
    loop_length,
    lat_order,
    wave_number,
):
    groups = lax.axis_size("band")
    band_index = lax.axis_index("band")
    loop_count, field_count, loop_width = grid_in.shape
    slot_count = legendre.shape[0]
    lat_count = lat_order.shape[0]
    half_count = lat_count // 2
    column_count = 2 * field_count
    wave_total = wave_number.shape[0]
    own_rows = lax.dynamic_slice_in_dim(lat_order, band_index * loop_count, loop_count)
    own_lengths = jnp.take(loop_length, own_rows)
    column_waves = wave_number.reshape(groups, slot_count).T.reshape(wave_total)
    own_waves = lax.dynamic_slice_in_dim(wave_number, band_index * slot_count, slot_count)

    def forward_piece(scan_carry, scan_item):
        one_loop, length = scan_item
        loop_piece = forward_loop(one_loop, length, column_waves).reshape(
            slot_count, groups, column_count
        )
        return (
            scan_carry,
            lax.all_to_all(loop_piece, "band", split_axis=1, concat_axis=1, tiled=True),
        )

    unused, pieces = lax.scan(forward_piece, 0, (grid_in, own_lengths))
    arrived = jnp.transpose(pieces, (1, 2, 0, 3))
    arrived = arrived.reshape(slot_count, lat_count, column_count)
    row_of_lat = jnp.argsort(lat_order)
    northern = jnp.take(arrived, row_of_lat[:half_count], axis=1).astype(jnp.float32)
    southern = jnp.take(arrived, row_of_lat[::-1][:half_count], axis=1).astype(jnp.float32)
    weight = gauss_weight[None, :, None]
    even_part = (weight * (northern + southern)).astype(jnp.bfloat16)
    odd_part = (weight * (northern - southern)).astype(jnp.bfloat16)
    stacked = jnp.stack([even_part, odd_part], axis=1)
    spectral = jnp.einsum("kprj,kpjc->kprc", legendre, stacked, preferred_element_type=jnp.float32)
    updated = semi_implicit(spectral, own_waves, vertical_modes, coupling, mode_rates)
    summed = jnp.einsum("kprj,kprc->kpjc", legendre, updated, preferred_element_type=jnp.float32)
    northern_back = summed[:, 0] + summed[:, 1]
    southern_back = summed[:, 0] - summed[:, 1]
    by_lat = jnp.concatenate([northern_back, southern_back[:, ::-1]], axis=1)
    resolved = 2 * own_waves[:, None] < loop_length[None, :]
    by_lat = jnp.where(resolved[:, :, None], by_lat, 0.0).astype(jnp.bfloat16)
    returning = jnp.take(by_lat, lat_order, axis=1).reshape(
        slot_count, groups, loop_count, column_count
    )
    outgoing_loops = jnp.transpose(returning, (2, 0, 1, 3))

    def inverse_piece(scan_carry, scan_item):
        loop_data, length = scan_item
        loop_back = lax.all_to_all(loop_data, "band", split_axis=1, concat_axis=1, tiled=True)
        return (
            scan_carry,
            inverse_loop(
                loop_back.reshape(wave_total, column_count), length, column_waves, loop_width
            ),
        )

    unused, grid_out = lax.scan(inverse_piece, 0, (outgoing_loops, own_lengths))
    return grid_out


def solution(mesh):
    placed = (
        P(("member", "band"), None, None),
        P("band", None, None, None),
        P(),
        P(),
        P(),
        P(),
        P(),
        P(),
        P(),
    )
    return jax.shard_map(
        per_device,
        mesh=mesh,
        in_specs=placed,
        out_specs=P(("member", "band"), None, None),
        check_vma=False,
    )
```

profile of v0, /device:TPU:0, one launch (start us, length us, event | category | flops | bytes accessed | tf_op | source)
XLA Modules:
  0.0 72.8 jit_solution(2726533253867949105)
XLA Ops:
  0.0 1.3 %dynamic_slice.17 = s32[1]{0:T(128)} dynamic-slice(s32[16]{0:T(128)} %param.18, s32[]{:T(128)S(6)} %select_n.129), dynamic_slice_sizes={1} | dynamic-slice | bytes 12 | tf_op jit(solution)/shard_map/dynamic_slice | solution.py:112
  3.2 1.3 %dynamic-slice.3 = s32[1]{0:T(128)} dynamic-slice(s32[16]{0:T(128)} %param.17, s32[]{:T(128)} %bitcast), dynamic_slice_sizes={1} | dynamic-slice | bytes 12 | tf_op jit(solution)/shard_map/jit(_take)/gather | solution.py:113
  5.3 0.5 iota_multiply_fusion.1
  5.8 3.7 %broadcast_select_fusion = bf16[1,274,5248]{2,1,0:T(8,128)(2,1)} fusion(bf16[1,274,5248]{2,1,0:T(8,128)(2,1)} %param.11, pred[5248]{0:T(1024)(128)(4,1)S(1)} %iota_compare_fusion), kind=kLoop, calls=%fused_computation.6 | loop fusion | flops 1437952 | bytes 5757056 | tf_op jit(solution)/shard_map/while/body/eval_jaxpr/jit(_where)/select_n | solution.py:29
  9.4 4.2 %select_n.136 = bf16[274,41,128]{2,1,0:T(8,128)(2,1)S(1)} reshape(bf16[1,274,5248]{2,1,0:T(8,128)(2,1)} %broadcast_select_fusion) | data formatting | bytes 5751808 | tf_op jit(solution)/shard_map/while/body/eval_jaxpr/jit(_where)/select_n | solution.py:29
  13.6 0.5 multiply_compare_fusion
  14.1 0.2 cosine_convert_fusion
  14.4 1.1 %fusion.46 = (f32[41,16]{1,0:T(8,128)S(1)}, f32[41,16]{1,0:T(8,128)S(1)}) fusion(f32[]{:T(128)S(6)} %convert_element_type.103, pred[]{:T(512)S(6)} %lt.94, s32[]{:T(128)S(6)} %select_n.133, s32[16]{0:T(128)} %param.19, s32[41]{0:T(128)} %iota_multiply_fusion.1), kind=kLoop, calls=%fused_computation.77 | loop fusion | flops 7216 | bytes 5485 | tf_op jit(solution)/shard_map/while/body/eval_jaxpr/cos | solution.py:20
  15.5 1.6 %fusion = f32[274,41,2,16]{0,3,2,1:T(8,128)S(1)} fusion(bf16[2,16,128,1]{2,1,0,3:T(8,128)(2,1)S(1)} %bitcast.133, bf16[274,41,128,1]{2,1,0,3:T(8,128)(2,1)S(1)} %bitcast.123), kind=kOutput, calls=%fused_computation.4 | convolution fusion | flops 92028928 | bytes 4322048 | tf_op jit(solution)/shard_map/while/body/eval_jaxpr/dot_general | solution.py:30
  17.1 0.0 copy-start.9
  17.1 0.0 copy-start.10
  17.1 0.0 copy-start.6
  17.1 0.0 copy-start.11
  17.1 0.0 copy-start.7
  17.2 0.0 copy-start.4
  17.2 0.4 subtract_reduce_fusion
  17.6 0.1 copy-done.9
  17.8 0.1 fusion.40
  17.9 0.5 broadcast.442
  18.4 0.7 reduce
  19.1 0.7 reshape.543
  19.8 7.4 %all-to-all-start = ((bf16[16,2,274]{2,1,0:T(2,128)(2,1)}), bf16[16,2,274]{2,1,0:T(2,128)(2,1)S(1)}, u32[]{:S(2)}, u32[]{:S(2)}) async-start(bf16[16,2,274]{2,1,0:T(2,128)(2,1)} %reshape.543), calls=%async_computation | async-start | bytes 49152 | tf_op jit(solution)/shard_map/while/body/eval_jaxpr/all_to_all | solution.py:124
  27.2 1.3 %sort.17 = (s32[16]{0:T(128)}, s32[16]{0:T(128)S(1)}) sort(s32[16]{0:T(128)S(1)} %copy-done.10, s32[16]{0:T(128)S(1)} %iota.42), dimensions={0}, to_apply=%region_2.3 | sort | flops 64 | bytes 256 | tf_op jit(solution)/shard_map/jit(argsort)/sort | solution.py:130
  28.5 0.1 slice.44
  28.6 0.1 slice.45
  28.7 0.7 dynamic_slice.18
  29.4 0.7 iota_add_fusion
  30.1 0.1 add_compare_fusion
  30.2 0.1 fusion.57
  31.0 0.1 multiply_add_fusion
  31.1 2.6 %all-to-all-done = bf16[16,2,274]{2,1,0:T(2,128)(2,1)S(1)} async-done(((bf16[16,2,274]{2,1,0:T(2,128)(2,1)}), bf16[16,2,274]{2,1,0:T(2,128)(2,1)S(1)}, u32[]{:S(2)}, u32[]{:S(2)}) %all-to-all-start) | async-done | bytes 17568 | tf_op jit(solution)/shard_map/while/body/eval_jaxpr/all_to_all | solution.py:124
  33.8 0.1 reshape.544
  33.9 0.6 gather_fusion.1
  34.5 0.6 gather_fusion.2
  35.0 0.1 fusion.48
  35.1 0.6 select_bitcast_fusion
  35.8 1.4 %copy.35 = f32[2,640,548]{1,0,2:T(2,128)S(1)} copy(f32[2,640,548]{1,2,0:T(8,128)S(1)} %select_bitcast_fusion) | data formatting | bytes 5611520 | tf_op jit(solution)/shard_map/jit(_where)/select_n | solution.py:74
  37.2 1.0 %fusion.60 = (f32[1,2,640,2,1,137]{2,1,5,4,3,0:T(2,128)S(1)}, f32[1,2,640,2,1,137]{2,1,5,4,3,0:T(2,128)S(1)}) fusion(f32[1,2,640,2,2,137]{2,1,5,4,3,0:T(2,128)S(1)} %bitcast.124), kind=kLoop, calls=%fused_computation.115 | loop fusion | bytes 5611520 | tf_op jit(solution)/shard_map/slice | solution.py:78
  38.2 1.4 %fusion.8 = f32[2,640,2,137]{1,3,2,0:T(8,128)S(1)} fusion(f32[1,2,640,2,1,137]{2,1,5,4,3,0:T(2,128)S(1)} %get-tuple-element.53, f32[137,137]{1,0:T(8,128)S(1)} %copy-done.1), kind=kOutput, calls=%fused_computation.17 | convolution fusion | flops 576583680 | bytes 2880836 | tf_op jit(solution)/shard_map/...l,kl->...k/dot_general | solution.py:80
  39.7 1.6 %fusion.3 = f32[2,640,2,137]{1,3,2,0:T(8,128)S(1)} fusion(f32[1,2,640,2,1,137]{2,1,5,4,3,0:T(2,128)S(1)} %get-tuple-element.54, f32[2,640,2,137]{1,3,2,0:T(8,128)S(1)} %fusion.8, f32[2,640]{1,0:T(2,128)S(1)} %fusion.57, f32[137,137]{1,0:T(8,128)S(1)} %copy-done), kind=kOutput, calls=%fused_computation.12 | convolution fusion | flops 577285120 | bytes 4288836 | tf_op jit(solution)/shard_map/...l,lk->...k/dot_general | solution.py:83
  41.3 1.6 %fusion.5 = f32[2,640,2,137]{1,3,2,0:T(8,128)S(1)} fusion(f32[2,640,2,137]{1,3,2,0:T(8,128)S(1)} %fusion.3, f32[2,640,137]{1,2,0:T(8,128)S(1)} %multiply_add_fusion, f32[137,137]{1,0:T(8,128)S(1)} %copy-done), kind=kOutput, calls=%fused_computation.14 | convolution fusion | flops 576934400 | bytes 3582276 | tf_op jit(solution)/shard_map/...k,lk->...l/dot_general | solution.py:85
  42.9 0.1 convert_bitcast_fusion
  43.0 1.5 %fusion.11 = bf16[1,2,640,2,1,137]{2,5,3,1,4,0:T(8,128)(2,1)S(1)} fusion(f32[2,640,2,137]{1,3,2,0:T(8,128)S(1)} %fusion.5, f32[1,2,640,2,1,137]{2,1,5,4,3,0:T(2,128)S(1)} %get-tuple-element.53, f32[137,137]{1,0:T(8,128)S(1)} %copy-done.1), kind=kOutput, calls=%fused_computation.20 | convolution fusion | flops 577635840 | bytes 3582276 | tf_op jit(solution)/shard_map/...l,kl->...k/dot_general | solution.py:86
  44.5 0.2 pad_maximum_fusion
  44.7 1.1 %copy.39 = bf16[1,2,640,2,2,137]{2,1,5,4,3,0:T(2,128)(2,1)S(1)} copy(bf16[1,2,640,2,2,137]{2,5,3,1,4,0:T(8,128)(2,1)S(1)} %pad_maximum_fusion) | data formatting | bytes 2805760 | tf_op jit(solution)/shard_map/stack | solution.py:89
  45.8 0.5 fusion.12
  46.3 0.1 rev.4
  46.4 0.1 fusion.39
  46.5 0.6 gather_fusion
  47.1 0.1 bitcast_select_fusion
  47.2 0.7 reduce.1
  47.9 0.7 reshape.545
  48.6 3.7 %all-to-all-start.1 = ((bf16[16,2,274]{2,1,0:T(2,128)(2,1)}), bf16[16,2,274]{2,1,0:T(2,128)(2,1)S(1)}, u32[]{:S(2)}, u32[]{:S(2)}) async-start(bf16[16,2,274]{2,1,0:T(2,128)(2,1)} %reshape.545), calls=%async_computation.1 | async-start | bytes 49152 | tf_op jit(solution)/shard_map/while/body/eval_jaxpr/all_to_all | solution.py:152
  52.3 6.3 %all-to-all-done.1 = bf16[16,2,274]{2,1,0:T(2,128)(2,1)S(1)} async-done(((bf16[16,2,274]{2,1,0:T(2,128)(2,1)}), bf16[16,2,274]{2,1,0:T(2,128)(2,1)S(1)}, u32[]{:S(2)}, u32[]{:S(2)}) %all-to-all-start.1) | async-done | bytes 17568 | tf_op jit(solution)/shard_map/while/body/eval_jaxpr/all_to_all | solution.py:152
  58.6 0.1 reshape.546
  58.7 0.1 multiply_bitcast_fusion.1
  58.8 0.3 subtract_convert_fusion.1
  59.2 0.9 %copy.43 = bf16[274,41,16]{1,0,2:T(8,128)(2,1)S(1)} copy(bf16[274,41,16]{0,2,1:T(8,128)(2,1)S(1)} %get-tuple-element.56) | data formatting | bytes 718976 | tf_op jit(solution)/shard_map/convert.2
  60.1 0.7 neg.14
  60.7 0.9 %copy.42 = bf16[274,41,16]{1,0,2:T(8,128)(2,1)S(1)} copy(bf16[274,41,16]{0,2,1:T(8,128)(2,1)S(1)} %get-tuple-element.55) | data formatting | bytes 718976 | tf_op jit(solution)/shard_map/convert.3
  61.6 0.7 sub.44
  62.3 3.3 %fusion.17 = bf16[11234,128]{1,0:T(8,128)(2,1)} fusion(bf16[11234,16]{0,1:T(8,128)(2,1)S(1)} %neg.14, bf16[11234,16]{0,1:T(8,128)(2,1)S(1)} %sub.44, bf16[128,16]{0,1:T(8,128)(2,1)S(1)} %get-tuple-element.66, bf16[128,16]{0,1:T(8,128)(2,1)S(1)} %get-tuple-element.65), kind=kOutput, calls=%fused_computation.32 | convolution fusion | flops 93483264 | bytes 3603072 | tf_op jit(solution)/shard_map/while/body/eval_jaxpr/dot_general | solution.py:56
  65.6 5.2 %reshape.469 = bf16[1,274,5248]{2,1,0:T(8,128)(2,1)S(1)} reshape(bf16[11234,128]{1,0:T(8,128)(2,1)} %fusion.17) | data formatting | bytes 5751808 | tf_op jit(solution)/shard_map/while/body/eval_jaxpr/reshape | solution.py:62
  70.7 2.1 %select_convert_fusion = bf16[1,274,5248]{2,1,0:T(8,128)(2,1)} fusion(bf16[1,274,5248]{2,1,0:T(8,128)(2,1)S(1)} %reshape.469, pred[5248]{0:T(1024)(128)(4,1)S(1)} %iota_compare_fusion), kind=kLoop, calls=%fused_computation.3 | loop fusion | flops 1437952 | bytes 5757056 | tf_op jit(solution)/shard_map/while/body/eval_jaxpr/convert_element_type | solution.py:64
  (36 shorter events, 0.2 us)
Async XLA Ops:
  0.0 39.7 %copy-start = (f32[137,137]{1,0:T(8,128)S(1)}, f32[137,137]{1,0:T(8,128)}, u32[]{:S(2)}) copy-start(f32[137,137]{1,0:T(8,128)} %param.14) | copy-start | bytes 225232
  9.4 4.2 %copy-start.5 = (s32[16]{0:T(128)S(1)}, s32[16]{0:T(128)}, u32[]{:S(2)}) copy-start(s32[16]{0:T(128)} %param.19) | copy-start | bytes 196
  15.5 1.7 %copy-start.2 = (f32[41,16]{1,0:T(8,128)}, f32[41,16]{1,0:T(8,128)S(1)}, u32[]{:S(2)}) copy-start(f32[41,16]{1,0:T(8,128)S(1)} %get-tuple-element.64) | copy-start | bytes 7876
  17.1 0.7 copy-start.9
  17.1 10.1 %copy-start.10 = (s32[16]{0:T(128)S(1)}, s32[16]{0:T(128)}, u32[]{:S(2)}) copy-start(s32[16]{0:T(128)} %param.18) | copy-start | bytes 196
  17.1 11.6 %copy-start.6 = (s32[16]{0:T(128)S(1)}, s32[16]{0:T(128)}, u32[]{:S(2)}) copy-start(s32[16]{0:T(128)} %param.19) | copy-start | bytes 196
  17.1 13.8 %copy-start.11 = (s32[16]{0:T(128)S(1)}, s32[16]{0:T(128)}, u32[]{:S(2)}) copy-start(s32[16]{0:T(128)} %param.17) | copy-start | bytes 196
  17.1 13.8 %copy-start.7 = (f32[137]{0:T(256)S(1)}, f32[137]{0:T(256)}, u32[]{:S(2)}) copy-start(f32[137]{0:T(256)} %param.16) | copy-start | bytes 1648
  17.2 17.9 %copy-start.8 = (f32[8]{0:T(128)S(1)}, f32[8]{0:T(128)}, u32[]{:S(2)}) copy-start(f32[8]{0:T(128)} %param.13) | copy-start | bytes 100
  17.2 17.9 %copy-start.4 = (bf16[1,2,640,8]{2,3,1,0:T(8,128)(2,1)S(1)}, bf16[1,2,640,8]{2,3,1,0:T(8,128)(2,1)}, u32[]{:S(2)}) copy-start(bf16[1,2,640,8]{2,3,1,0:T(8,128)(2,1)} %param.12) | copy-start | bytes 61444
  19.8 14.0 %all-to-all-start = ((bf16[16,2,274]{2,1,0:T(2,128)(2,1)}), bf16[16,2,274]{2,1,0:T(2,128)(2,1)S(1)}, u32[]{:S(2)}, u32[]{:S(2)}) async-start(bf16[16,2,274]{2,1,0:T(2,128)(2,1)} %reshape.543), calls=%async_computation | async-start | bytes 49152 | tf_op jit(solution)/shard_map/while/body/eval_jaxpr/all_to_all | solution.py:124
  37.2 1.0 %copy-start.1 = (f32[137,137]{1,0:T(8,128)S(1)}, f32[137,137]{1,0:T(8,128)}, u32[]{:S(2)}) copy-start(f32[137,137]{1,0:T(8,128)} %param.15) | copy-start | bytes 225232
  45.8 13.0 %copy-start.3 = (f32[41,16]{1,0:T(8,128)S(1)}, f32[41,16]{1,0:T(8,128)}, u32[]{:S(2)}) copy-start(f32[41,16]{1,0:T(8,128)} %copy-done.2) | copy-start | bytes 7876
  48.6 10.0 %all-to-all-start.1 = ((bf16[16,2,274]{2,1,0:T(2,128)(2,1)}), bf16[16,2,274]{2,1,0:T(2,128)(2,1)S(1)}, u32[]{:S(2)}, u32[]{:S(2)}) async-start(bf16[16,2,274]{2,1,0:T(2,128)(2,1)} %reshape.545), calls=%async_computation.1 | async-start | bytes 49152 | tf_op jit(solution)/shard_map/while/body/eval_jaxpr/all_to_all | solution.py:152
where the time goes:
time: 73.4 us; the launch traced here: 72.8 us
  local copies, waits for them, and re-layouts  23.6 us (32%)
  other arithmetic  13.2 us (18%)
  matrix products  12.1 us (16%)
  starting transfers between devices  11.1 us (15%)
  waiting for transfers between devices  8.92 us (12%)
  between operations  3.86 us (5%)
    all_to_all x1, starting transfers between devices, forward_piece(): lax.all_to_all(loop_piece, 'band', split_axis=1, concat_axis=1, tiled=True)  7.42 us
    all_to_all x1, waiting for transfers between devices, inverse_piece(): lax.all_to_all(loop_data, 'band', split_axis=1, concat_axis=1, tiled=True)  6.3 us
    reshape x1, local copies, waits for them, and re-layouts, inverse_loop(): points = points.reshape(field_count, loop_width)  5.17 us
    select_n x1, local copies, waits for them, and re-layouts, forward_loop(): masked = jnp.where(inside[None, :], one_loop, jnp.zeros((), one_loop.dtype))  4.15 us
    all_to_all x1, starting transfers between devices, inverse_piece(): lax.all_to_all(loop_data, 'band', split_axis=1, concat_axis=1, tiled=True)  3.72 us
    select_n x1, other arithmetic, forward_loop(): masked = jnp.where(inside[None, :], one_loop, jnp.zeros((), one_loop.dtype))  3.66 us
    dot_general x1, matrix products, inverse_loop(): lax.dot_general(combined.reshape(field_count * block_count, 2 * wave_coun...  3.28 us
    all_to_all x1, waiting for transfers between devices, forward_piece(): lax.all_to_all(loop_piece, 'band', split_axis=1, concat_axis=1, tiled=True)  2.62 us
  transfers between devices with their start and end apart: 2, of which 2 were waited for; matrix products, arithmetic and copies ran while one was open for 4% of the time, Pallas kernels for 0%

commit v1 on v0

--- a/solution.py
+++ b/solution.py
@@ -3,10 +3,27 @@
 import jax.numpy as jnp
 from jax import lax
 from jax.sharding import PartitionSpec as P
+from jax.lax import axis_index, axis_size, ppermute
 
 TRUNC = 1279
 implicit_step = 0.5
 highest = lax.Precision.HIGHEST
+
+
+def tell_hubs(local_x, dim_no, base_x):
+    after = local_x.shape
+    o_now = local_x.reshape(*after[:dim_no], base_x, after[dim_no] // base_x, *after[dim_no + 1 :])
+    side_arr = jnp.moveaxis(o_now, dim_no, 0)
+    return side_arr
+
+
+def make_windows(shard_in, array_axis):
+    shard_in = jnp.moveaxis(shard_in, 0, array_axis)
+    v_now = shard_in.shape
+    moved = shard_in.reshape(
+        *v_now[:array_axis], v_now[array_axis] * v_now[array_axis + 1], *v_now[array_axis + 2 :]
+    )
+    return moved
 
 
 def loop_tables(length, wave_list, block_count):
@@ -149,7 +166,22 @@
 
     def inverse_piece(scan_carry, scan_item):
         loop_data, length = scan_item
-        loop_back = lax.all_to_all(loop_data, "band", split_axis=1, concat_axis=1, tiled=True)
+
+        def connect_limits(values, which_axis, arr, matrix):
+            heard = axis_size(which_axis)
+            piece_now, tall = (heard, axis_index(which_axis))
+            top = tell_hubs(values, arr, piece_now)
+            local_next = top
+            for h in range(1, piece_now):
+                x_now, passed = ((tall + h) % piece_now, (tall - h) % piece_now)
+                lower = lax.dynamic_index_in_dim(top, x_now, 0)
+                state_next = tuple(((d, (d + h) % piece_now) for d in range(piece_now)))
+                v_next = ppermute(lower, which_axis, state_next)
+                local_next = lax.dynamic_update_slice_in_dim(local_next, v_next, passed, axis=0)
+            latest = make_windows(local_next, matrix)
+            return latest
+
+        loop_back = connect_limits(loop_data, "band", 1, 1)
         return (
             scan_carry,
             inverse_loop(

time: 73.4 us -> 85.1 us (1.16)
  starting transfers between devices: 11.1 us -> 26.4 us
  waiting for transfers between devices: 8.92 us -> 5.16 us
    ppermute x0 -> x15, starting transfers between devices: none -> 18.9 us  [connect_limits(): v_next = ppermute(lower, which_axis, state_next)]
    all_to_all x1 -> x0, waiting for transfers between devices: 6.3 us -> none  [inverse_piece(): lax.all_to_all(loop_data, 'band', split_axis=1, concat_axis=1, tiled=True)]
    all_to_all x1 -> x0, starting transfers between devices: 3.72 us -> none  [inverse_piece(): lax.all_to_all(loop_data, 'band', split_axis=1, concat_axis=1, tiled=True)]
    ppermute x0 -> x15, waiting for transfers between devices: none -> 2.89 us  [connect_limits(): v_next = ppermute(lower, which_axis, state_next)]
    unnamed x31 -> x28, local copies, waits for them, and re-layouts: 2.35 us -> 1.55 us
  transfers between devices with their start and end apart: 2 -> 16, of which waited for: 2 -> 3; matrix products, arithmetic and copies ran while one was open for 4% -> 4% of each run, Pallas kernels for 0% -> 0%
where the time goes in v1:
time: 85.1 us; the launch traced here: 84.2 us
  starting transfers between devices  26.4 us (31%)
  local copies, waits for them, and re-layouts  23.5 us (28%)
  other arithmetic  12.6 us (15%)
  matrix products  12.1 us (14%)
  waiting for transfers between devices  5.16 us (6%)
  between operations  4.45 us (5%)
    ppermute x15, starting transfers between devices, connect_limits(): v_next = ppermute(lower, which_axis, state_next)  18.9 us
    all_to_all x1, starting transfers between devices, forward_piece(): lax.all_to_all(loop_piece, 'band', split_axis=1, concat_axis=1, tiled=True)  7.42 us
    reshape x1, local copies, waits for them, and re-layouts, inverse_loop(): points = points.reshape(field_count, loop_width)  5.17 us
    select_n x1, local copies, waits for them, and re-layouts, forward_loop(): masked = jnp.where(inside[None, :], one_loop, jnp.zeros((), one_loop.dtype))  4.15 us
    select_n x1, other arithmetic, forward_loop(): masked = jnp.where(inside[None, :], one_loop, jnp.zeros((), one_loop.dtype))  3.66 us
    dot_general x1, matrix products, inverse_loop(): lax.dot_general(combined.reshape(field_count * block_count, 2 * wave_coun...  3.28 us
    ppermute x15, waiting for transfers between devices, connect_limits(): v_next = ppermute(lower, which_axis, state_next)  2.89 us
    all_to_all x1, waiting for transfers between devices, forward_piece(): lax.all_to_all(loop_piece, 'band', split_axis=1, concat_axis=1, tiled=True)  2.28 us
  transfers between devices with their start and end apart: 16, of which 3 were waited for; matrix products, arithmetic and copies ran while one was open for 4% of the time, Pallas kernels for 0%

profile of v1, /device:TPU:0, one launch (start us, length us, event | category | flops | bytes accessed | tf_op | source)
XLA Modules:
  0.0 84.2 jit_solution(14174149198128723278)
XLA Ops:
  0.0 1.3 %dynamic_slice.108 = s32[1]{0:T(128)} dynamic-slice(s32[16]{0:T(128)} %param.18, s32[]{:T(128)S(6)} %select_n.409), dynamic_slice_sizes={1} | dynamic-slice | bytes 12 | tf_op jit(solution)/shard_map/dynamic_slice | solution.py:129
  3.2 1.3 %dynamic-slice.18 = s32[1]{0:T(128)} dynamic-slice(s32[16]{0:T(128)} %param.17, s32[]{:T(128)} %bitcast), dynamic_slice_sizes={1} | dynamic-slice | bytes 12 | tf_op jit(solution)/shard_map/jit(_take)/gather | solution.py:130
  5.2 0.5 iota_multiply_fusion.1
  5.7 3.7 %broadcast_select_fusion = bf16[1,274,5248]{2,1,0:T(8,128)(2,1)} fusion(bf16[1,274,5248]{2,1,0:T(8,128)(2,1)} %param.11, pred[5248]{0:T(1024)(128)(4,1)S(1)} %iota_compare_fusion), kind=kLoop, calls=%fused_computation.6 | loop fusion | flops 1437952 | bytes 5757056 | tf_op jit(solution)/shard_map/while/body/eval_jaxpr/jit(_where)/select_n | solution.py:46
  9.4 4.2 %select_n.416 = bf16[274,41,128]{2,1,0:T(8,128)(2,1)S(1)} reshape(bf16[1,274,5248]{2,1,0:T(8,128)(2,1)} %broadcast_select_fusion) | data formatting | bytes 5751808 | tf_op jit(solution)/shard_map/while/body/eval_jaxpr/jit(_where)/select_n | solution.py:46
  13.6 0.5 multiply_compare_fusion
  14.1 0.2 cosine_convert_fusion
  14.3 1.1 %fusion.46 = (f32[41,16]{1,0:T(8,128)S(1)}, f32[41,16]{1,0:T(8,128)S(1)}) fusion(f32[]{:T(128)S(6)} %convert_element_type.103, pred[]{:T(512)S(6)} %lt.368, s32[]{:T(128)S(6)} %select_n.413, s32[16]{0:T(128)} %param.19, s32[41]{0:T(128)} %iota_multiply_fusion.1), kind=kLoop, calls=%fused_computation.77 | loop fusion | flops 7216 | bytes 5485 | tf_op jit(solution)/shard_map/while/body/eval_jaxpr/cos | solution.py:37
  15.5 1.6 %fusion = f32[274,41,2,16]{0,3,2,1:T(8,128)S(1)} fusion(bf16[2,16,128,1]{2,1,0,3:T(8,128)(2,1)S(1)} %bitcast.168, bf16[274,41,128,1]{2,1,0,3:T(8,128)(2,1)S(1)} %bitcast.161), kind=kOutput, calls=%fused_computation.4 | convolution fusion | flops 92028928 | bytes 4322048 | tf_op jit(solution)/shard_map/while/body/eval_jaxpr/dot_general | solution.py:47
  17.1 0.4 subtract_reduce_fusion
  17.6 0.2 copy-done.9
  17.7 0.1 fusion.40
  17.8 0.5 broadcast.482
  18.4 0.8 reduce
  19.1 0.7 reshape.600
  19.8 7.4 %all-to-all-start = ((bf16[16,2,274]{2,1,0:T(2,128)(2,1)}), bf16[16,2,274]{2,1,0:T(2,128)(2,1)S(1)}, u32[]{:S(2)}, u32[]{:S(2)}) async-start(bf16[16,2,274]{2,1,0:T(2,128)(2,1)} %reshape.600), calls=%async_computation | async-start | bytes 49152 | tf_op jit(solution)/shard_map/while/body/eval_jaxpr/all_to_all | solution.py:141
  27.3 1.3 %sort.17 = (s32[16]{0:T(128)}, s32[16]{0:T(128)S(1)}) sort(s32[16]{0:T(128)S(1)} %copy-done.10, s32[16]{0:T(128)S(1)} %iota.42), dimensions={0}, to_apply=%region_2.3 | sort | flops 64 | bytes 256 | tf_op jit(solution)/shard_map/jit(argsort)/sort | solution.py:147
  28.6 0.1 slice.45
  28.7 0.6 dynamic_slice.109
  29.3 0.6 iota_add_fusion
  30.8 0.1 multiply_add_fusion
  31.5 2.3 %all-to-all-done = bf16[16,2,274]{2,1,0:T(2,128)(2,1)S(1)} async-done(((bf16[16,2,274]{2,1,0:T(2,128)(2,1)}), bf16[16,2,274]{2,1,0:T(2,128)(2,1)S(1)}, u32[]{:S(2)}, u32[]{:S(2)}) %all-to-all-start) | async-done | bytes 17568 | tf_op jit(solution)/shard_map/while/body/eval_jaxpr/all_to_all | solution.py:141
  33.8 0.1 reshape.601
  33.9 0.6 gather_fusion.1
  34.5 0.6 gather_fusion.2
  35.1 0.1 fusion.48
  35.2 0.6 select_bitcast_fusion
  35.8 1.4 %copy.34 = f32[2,640,548]{1,0,2:T(2,128)S(1)} copy(f32[2,640,548]{1,2,0:T(8,128)S(1)} %select_bitcast_fusion) | data formatting | bytes 5611520 | tf_op jit(solution)/shard_map/jit(_where)/select_n | solution.py:91
  37.3 1.0 %fusion.75 = (f32[1,2,640,2,1,137]{2,1,5,4,3,0:T(2,128)S(1)}, f32[1,2,640,2,1,137]{2,1,5,4,3,0:T(2,128)S(1)}) fusion(f32[1,2,640,2,2,137]{2,1,5,4,3,0:T(2,128)S(1)} %bitcast.162), kind=kLoop, calls=%fused_computation.145 | loop fusion | bytes 5611520 | tf_op jit(solution)/shard_map/slice | solution.py:95
  38.3 1.4 %fusion.8 = f32[2,640,2,137]{1,3,2,0:T(8,128)S(1)} fusion(f32[1,2,640,2,1,137]{2,1,5,4,3,0:T(2,128)S(1)} %get-tuple-element.53, f32[137,137]{1,0:T(8,128)S(1)} %copy-done.1), kind=kOutput, calls=%fused_computation.17 | convolution fusion | flops 576583680 | bytes 2880836 | tf_op jit(solution)/shard_map/...l,kl->...k/dot_general | solution.py:97
  39.7 1.6 %fusion.3 = f32[2,640,2,137]{1,3,2,0:T(8,128)S(1)} fusion(f32[1,2,640,2,1,137]{2,1,5,4,3,0:T(2,128)S(1)} %get-tuple-element.54, f32[2,640,2,137]{1,3,2,0:T(8,128)S(1)} %fusion.8, f32[2,640]{1,0:T(2,128)S(1)} %fusion.57, f32[137,137]{1,0:T(8,128)S(1)} %copy-done), kind=kOutput, calls=%fused_computation.12 | convolution fusion | flops 577285120 | bytes 4288836 | tf_op jit(solution)/shard_map/...l,lk->...k/dot_general | solution.py:100
  41.3 1.6 %fusion.5 = f32[2,640,2,137]{1,3,2,0:T(8,128)S(1)} fusion(f32[2,640,2,137]{1,3,2,0:T(8,128)S(1)} %fusion.3, f32[2,640,137]{1,2,0:T(8,128)S(1)} %multiply_add_fusion, f32[137,137]{1,0:T(8,128)S(1)} %copy-done), kind=kOutput, calls=%fused_computation.14 | convolution fusion | flops 576934400 | bytes 3582276 | tf_op jit(solution)/shard_map/...k,lk->...l/dot_general | solution.py:102
  42.9 0.1 convert_bitcast_fusion
  43.0 1.5 %fusion.11 = bf16[1,2,640,2,1,137]{2,5,3,1,4,0:T(8,128)(2,1)S(1)} fusion(f32[2,640,2,137]{1,3,2,0:T(8,128)S(1)} %fusion.5, f32[1,2,640,2,1,137]{2,1,5,4,3,0:T(2,128)S(1)} %get-tuple-element.53, f32[137,137]{1,0:T(8,128)S(1)} %copy-done.1), kind=kOutput, calls=%fused_computation.20 | convolution fusion | flops 577635840 | bytes 3582276 | tf_op jit(solution)/shard_map/...l,kl->...k/dot_general | solution.py:103
  44.6 0.2 pad_maximum_fusion
  44.7 1.1 %copy.38 = bf16[1,2,640,2,2,137]{2,1,5,4,3,0:T(2,128)(2,1)S(1)} copy(bf16[1,2,640,2,2,137]{2,5,3,1,4,0:T(8,128)(2,1)S(1)} %pad_maximum_fusion) | data formatting | bytes 2805760 | tf_op jit(solution)/shard_map/stack | solution.py:106
  45.8 0.5 fusion.12
  46.3 0.1 rev.4
  46.5 0.6 gather_fusion
  47.1 0.1 bitcast_select_fusion
  47.3 0.3 collective-permute-start
  47.6 0.5 collective-permute-start.1
  48.1 1.5 %collective-permute-start.2 = (bf16[1,1,1,548]{3,2,1,0:T(2,128)(2,1)S(1)}, bf16[1,1,1,548]{3,2,1,0:T(2,128)(2,1)S(1)}, u32[]{:S(2)}, u32[]{:S(2)}) collective-permute-start(bf16[1,1,1,548]{3,2,1,0:T(2,128)(2,1)S(1)} %get-tuple-element.75), channel_id=1, source_target_pairs={{0,3},{1,4},{2,5},{3,6},{4,7},{5,8},{6,9},{7,10},{8,11},{9,12},{10... | collective-permute-start | bytes 3296 | tf_op jit(solution)/shard_map/while/body/eval_jaxpr/ppermute | solution.py:179
  49.6 1.5 %collective-permute-start.3 = (bf16[1,1,1,548]{3,2,1,0:T(2,128)(2,1)S(1)}, bf16[1,1,1,548]{3,2,1,0:T(2,128)(2,1)S(1)}, u32[]{:S(2)}, u32[]{:S(2)}) collective-permute-start(bf16[1,1,1,548]{3,2,1,0:T(2,128)(2,1)S(1)} %get-tuple-element.74), channel_id=1, source_target_pairs={{0,4},{1,5},{2,6},{3,7},{4,8},{5,9},{6,10},{7,11},{8,12},{9,13},{1... | collective-permute-start | bytes 3296 | tf_op jit(solution)/shard_map/while/body/eval_jaxpr/ppermute | solution.py:179
  51.1 0.1 collective-permute-start.4
  51.2 2.0 %collective-permute-done = bf16[1,1,1,548]{3,2,1,0:T(2,128)(2,1)S(1)} collective-permute-done((bf16[1,1,1,548]{3,2,1,0:T(2,128)(2,1)S(1)}, bf16[1,1,1,548]{3,2,1,0:T(2,128)(2,1)S(1)}, u32[]{:S(2)}, u32[]{:S(2)}) %collective-permute-start) | collective-permute-done | bytes 1128 | tf_op jit(solution)/shard_map/while/body/eval_jaxpr/ppermute | solution.py:179
  53.3 1.2 %collective-permute-start.5 = (bf16[1,1,1,548]{3,2,1,0:T(2,128)(2,1)S(1)}, bf16[1,1,1,548]{3,2,1,0:T(2,128)(2,1)S(1)}, u32[]{:S(2)}, u32[]{:S(2)}) collective-permute-start(bf16[1,1,1,548]{3,2,1,0:T(2,128)(2,1)S(1)} %get-tuple-element.72), channel_id=1, source_target_pairs={{0,6},{1,7},{2,8},{3,9},{4,10},{5,11},{6,12},{7,13},{8,14},{9,15},... | collective-permute-start | bytes 3296 | tf_op jit(solution)/shard_map/while/body/eval_jaxpr/ppermute | solution.py:179
  54.5 2.4 %collective-permute-start.6 = (bf16[1,1,1,548]{3,2,1,0:T(2,128)(2,1)S(1)}, bf16[1,1,1,548]{3,2,1,0:T(2,128)(2,1)S(1)}, u32[]{:S(2)}, u32[]{:S(2)}) collective-permute-start(bf16[1,1,1,548]{3,2,1,0:T(2,128)(2,1)S(1)} %get-tuple-element.71), channel_id=1, source_target_pairs={{0,7},{1,8},{2,9},{3,10},{4,11},{5,12},{6,13},{7,14},{8,15},{9,0},... | collective-permute-start | bytes 3296 | tf_op jit(solution)/shard_map/while/body/eval_jaxpr/ppermute | solution.py:179
  56.8 1.3 %collective-permute-start.7 = (bf16[1,1,1,548]{3,2,1,0:T(2,128)(2,1)S(1)}, bf16[1,1,1,548]{3,2,1,0:T(2,128)(2,1)S(1)}, u32[]{:S(2)}, u32[]{:S(2)}) collective-permute-start(bf16[1,1,1,548]{3,2,1,0:T(2,128)(2,1)S(1)} %get-tuple-element.70), channel_id=1, source_target_pairs={{0,8},{1,9},{2,10},{3,11},{4,12},{5,13},{6,14},{7,15},{8,0},{9,1},... | collective-permute-start | bytes 3296 | tf_op jit(solution)/shard_map/while/body/eval_jaxpr/ppermute | solution.py:179
  58.1 2.3 %collective-permute-start.9 = (bf16[1,1,1,548]{3,2,1,0:T(2,128)(2,1)S(1)}, bf16[1,1,1,548]{3,2,1,0:T(2,128)(2,1)S(1)}, u32[]{:S(2)}, u32[]{:S(2)}) collective-permute-start(bf16[1,1,1,548]{3,2,1,0:T(2,128)(2,1)S(1)} %get-tuple-element.68), channel_id=1, source_target_pairs={{0,10},{1,11},{2,12},{3,13},{4,14},{5,15},{6,0},{7,1},{8,2},{9,3},... | collective-permute-start | bytes 3296 | tf_op jit(solution)/shard_map/while/body/eval_jaxpr/ppermute | solution.py:179
  60.7 3.4 %collective-permute-start.10 = (bf16[1,1,1,548]{3,2,1,0:T(2,128)(2,1)S(1)}, bf16[1,1,1,548]{3,2,1,0:T(2,128)(2,1)S(1)}, u32[]{:S(2)}, u32[]{:S(2)}) collective-permute-start(bf16[1,1,1,548]{3,2,1,0:T(2,128)(2,1)S(1)} %get-tuple-element.67), channel_id=1, source_target_pairs={{0,11},{1,12},{2,13},{3,14},{4,15},{5,0},{6,1},{7,2},{8,3},{9,4},{... | collective-permute-start | bytes 3296 | tf_op jit(solution)/shard_map/while/body/eval_jaxpr/ppermute | solution.py:179
  64.1 0.7 collective-permute-start.11
  64.8 0.7 collective-permute-start.12
  65.5 1.2 %collective-permute-start.13 = (bf16[1,1,1,548]{3,2,1,0:T(2,128)(2,1)S(1)}, bf16[1,1,1,548]{3,2,1,0:T(2,128)(2,1)S(1)}, u32[]{:S(2)}, u32[]{:S(2)}) collective-permute-start(bf16[1,1,1,548]{3,2,1,0:T(2,128)(2,1)S(1)} %get-tuple-element.64), channel_id=1, source_target_pairs={{0,14},{1,15},{2,0},{3,1},{4,2},{5,3},{6,4},{7,5},{8,6},{9,7},{10,... | collective-permute-start | bytes 3296 | tf_op jit(solution)/shard_map/while/body/eval_jaxpr/ppermute | solution.py:179
  66.7 1.9 %collective-permute-start.14 = (bf16[1,1,1,548]{3,2,1,0:T(2,128)(2,1)S(1)}, bf16[1,1,1,548]{3,2,1,0:T(2,128)(2,1)S(1)}, u32[]{:S(2)}, u32[]{:S(2)}) collective-permute-start(bf16[1,1,1,548]{3,2,1,0:T(2,128)(2,1)S(1)} %get-tuple-element.63), channel_id=1, source_target_pairs={{0,15},{1,0},{2,1},{3,2},{4,3},{5,4},{6,5},{7,6},{8,7},{9,8},{10,9... | collective-permute-start | bytes 3296 | tf_op jit(solution)/shard_map/while/body/eval_jaxpr/ppermute | solution.py:179
  69.1 0.8 collective-permute-done.14
  70.1 0.3 subtract_convert_fusion.1
  70.4 1.0 %copy.41 = bf16[274,41,16]{1,0,2:T(8,128)(2,1)S(1)} copy(bf16[274,41,16]{0,2,1:T(8,128)(2,1)S(1)} %get-tuple-element.56) | data formatting | bytes 718976 | tf_op jit(solution)/shard_map/convert.2
  71.4 0.7 neg.14
  72.0 1.0 %copy.40 = bf16[274,41,16]{1,0,2:T(8,128)(2,1)S(1)} copy(bf16[274,41,16]{0,2,1:T(8,128)(2,1)S(1)} %get-tuple-element.55) | data formatting | bytes 718976 | tf_op jit(solution)/shard_map/convert.3
  73.0 0.7 sub.119
  73.7 3.3 %fusion.17 = bf16[11234,128]{1,0:T(8,128)(2,1)} fusion(bf16[11234,16]{0,1:T(8,128)(2,1)S(1)} %neg.14, bf16[11234,16]{0,1:T(8,128)(2,1)S(1)} %sub.119, bf16[128,16]{0,1:T(8,128)(2,1)S(1)} %get-tuple-element.81, bf16[128,16]{0,1:T(8,128)(2,1)S(1)} %get-tuple-element.80), kind=kOutput, calls=%fused_computation.32 | convolution fusion | flops 93483264 | bytes 3603072 | tf_op jit(solution)/shard_map/while/body/eval_jaxpr/dot_general | solution.py:73
  76.9 5.2 %reshape.525 = bf16[1,274,5248]{2,1,0:T(8,128)(2,1)S(1)} reshape(bf16[11234,128]{1,0:T(8,128)(2,1)} %fusion.17) | data formatting | bytes 5751808 | tf_op jit(solution)/shard_map/while/body/eval_jaxpr/reshape | solution.py:79
  82.1 2.1 %select_convert_fusion = bf16[1,274,5248]{2,1,0:T(8,128)(2,1)} fusion(bf16[1,274,5248]{2,1,0:T(8,128)(2,1)S(1)} %reshape.525, pred[5248]{0:T(1024)(128)(4,1)S(1)} %iota_compare_fusion), kind=kLoop, calls=%fused_computation.3 | loop fusion | flops 1437952 | bytes 5757056 | tf_op jit(solution)/shard_map/while/body/eval_jaxpr/convert_element_type | solution.py:81
  (76 shorter events, 1.4 us)
Async XLA Ops:
  0.0 39.7 %copy-start = (f32[137,137]{1,0:T(8,128)S(1)}, f32[137,137]{1,0:T(8,128)}, u32[]{:S(2)}) copy-start(f32[137,137]{1,0:T(8,128)} %param.14) | copy-start | bytes 225232
  9.4 4.2 %copy-start.5 = (s32[16]{0:T(128)S(1)}, s32[16]{0:T(128)}, u32[]{:S(2)}) copy-start(s32[16]{0:T(128)} %param.19) | copy-start | bytes 196
  15.4 1.7 %copy-start.2 = (f32[41,16]{1,0:T(8,128)}, f32[41,16]{1,0:T(8,128)S(1)}, u32[]{:S(2)}) copy-start(f32[41,16]{1,0:T(8,128)S(1)} %get-tuple-element.79) | copy-start | bytes 7876
  17.1 0.7 copy-start.9
  17.1 10.2 %copy-start.10 = (s32[16]{0:T(128)S(1)}, s32[16]{0:T(128)}, u32[]{:S(2)}) copy-start(s32[16]{0:T(128)} %param.18) | copy-start | bytes 196
  17.1 11.6 %copy-start.6 = (s32[16]{0:T(128)S(1)}, s32[16]{0:T(128)}, u32[]{:S(2)}) copy-start(s32[16]{0:T(128)} %param.19) | copy-start | bytes 196
  17.1 13.7 %copy-start.11 = (s32[16]{0:T(128)S(1)}, s32[16]{0:T(128)}, u32[]{:S(2)}) copy-start(s32[16]{0:T(128)} %param.17) | copy-start | bytes 196
  17.1 13.7 %copy-start.7 = (f32[137]{0:T(256)S(1)}, f32[137]{0:T(256)}, u32[]{:S(2)}) copy-start(f32[137]{0:T(256)} %param.16) | copy-start | bytes 1648
  17.5 17.6 %copy-start.8 = (f32[8]{0:T(128)S(1)}, f32[8]{0:T(128)}, u32[]{:S(2)}) copy-start(f32[8]{0:T(128)} %param.13) | copy-start | bytes 100
  17.5 17.7 %copy-start.4 = (bf16[1,2,640,8]{2,3,1,0:T(8,128)(2,1)S(1)}, bf16[1,2,640,8]{2,3,1,0:T(8,128)(2,1)}, u32[]{:S(2)}) copy-start(bf16[1,2,640,8]{2,3,1,0:T(8,128)(2,1)} %param.12) | copy-start | bytes 61444
  19.8 14.0 %all-to-all-start = ((bf16[16,2,274]{2,1,0:T(2,128)(2,1)}), bf16[16,2,274]{2,1,0:T(2,128)(2,1)S(1)}, u32[]{:S(2)}, u32[]{:S(2)}) async-start(bf16[16,2,274]{2,1,0:T(2,128)(2,1)} %reshape.600), calls=%async_computation | async-start | bytes 49152 | tf_op jit(solution)/shard_map/while/body/eval_jaxpr/all_to_all | solution.py:141
  37.3 1.0 %copy-start.1 = (f32[137,137]{1,0:T(8,128)S(1)}, f32[137,137]{1,0:T(8,128)}, u32[]{:S(2)}) copy-start(f32[137,137]{1,0:T(8,128)} %param.15) | copy-start | bytes 225232
  45.8 24.2 %copy-start.3 = (f32[41,16]{1,0:T(8,128)S(1)}, f32[41,16]{1,0:T(8,128)}, u32[]{:S(2)}) copy-start(f32[41,16]{1,0:T(8,128)} %copy-done.2) | copy-start | bytes 7876
  47.3 6.0 %collective-permute-start = (bf16[1,1,1,548]{3,2,1,0:T(2,128)(2,1)S(1)}, bf16[1,1,1,548]{3,2,1,0:T(2,128)(2,1)S(1)}, u32[]{:S(2)}, u32[]{:S(2)}) collective-permute-start(bf16[1,1,1,548]{3,2,1,0:T(2,128)(2,1)S(1)} %get-tuple-element.77), channel_id=1, source_target_pairs={{0,1},{1,2},{2,3},{3,4},{4,5},{5,6},{6,7},{7,8},{8,9},{9,10},{10,1... | collective-permute-start | bytes 3296 | tf_op jit(solution)/shard_map/while/body/eval_jaxpr/ppermute | solution.py:179
  47.6 6.9 %collective-permute-start.1 = (bf16[1,1,1,548]{3,2,1,0:T(2,128)(2,1)S(1)}, bf16[1,1,1,548]{3,2,1,0:T(2,128)(2,1)S(1)}, u32[]{:S(2)}, u32[]{:S(2)}) collective-permute-start(bf16[1,1,1,548]{3,2,1,0:T(2,128)(2,1)S(1)} %get-tuple-element.76), channel_id=1, source_target_pairs={{0,2},{1,3},{2,4},{3,5},{4,6},{5,7},{6,8},{7,9},{8,10},{9,11},{10,... | collective-permute-start | bytes 3296 | tf_op jit(solution)/shard_map/while/body/eval_jaxpr/ppermute | solution.py:179
  48.1 8.8 %collective-permute-start.2 = (bf16[1,1,1,548]{3,2,1,0:T(2,128)(2,1)S(1)}, bf16[1,1,1,548]{3,2,1,0:T(2,128)(2,1)S(1)}, u32[]{:S(2)}, u32[]{:S(2)}) collective-permute-start(bf16[1,1,1,548]{3,2,1,0:T(2,128)(2,1)S(1)} %get-tuple-element.75), channel_id=1, source_target_pairs={{0,3},{1,4},{2,5},{3,6},{4,7},{5,8},{6,9},{7,10},{8,11},{9,12},{10... | collective-permute-start | bytes 3296 | tf_op jit(solution)/shard_map/while/body/eval_jaxpr/ppermute | solution.py:179
  49.6 8.5 %collective-permute-start.3 = (bf16[1,1,1,548]{3,2,1,0:T(2,128)(2,1)S(1)}, bf16[1,1,1,548]{3,2,1,0:T(2,128)(2,1)S(1)}, u32[]{:S(2)}, u32[]{:S(2)}) collective-permute-start(bf16[1,1,1,548]{3,2,1,0:T(2,128)(2,1)S(1)} %get-tuple-element.74), channel_id=1, source_target_pairs={{0,4},{1,5},{2,6},{3,7},{4,8},{5,9},{6,10},{7,11},{8,12},{9,13},{1... | collective-permute-start | bytes 3296 | tf_op jit(solution)/shard_map/while/body/eval_jaxpr/ppermute | solution.py:179
  51.1 7.1 %collective-permute-start.4 = (bf16[1,1,1,548]{3,2,1,0:T(2,128)(2,1)S(1)}, bf16[1,1,1,548]{3,2,1,0:T(2,128)(2,1)S(1)}, u32[]{:S(2)}, u32[]{:S(2)}) collective-permute-start(bf16[1,1,1,548]{3,2,1,0:T(2,128)(2,1)S(1)} %get-tuple-element.73), channel_id=1, source_target_pairs={{0,5},{1,6},{2,7},{3,8},{4,9},{5,10},{6,11},{7,12},{8,13},{9,14},{... | collective-permute-start | bytes 3296 | tf_op jit(solution)/shard_map/while/body/eval_jaxpr/ppermute | solution.py:179
  53.3 7.4 %collective-permute-start.5 = (bf16[1,1,1,548]{3,2,1,0:T(2,128)(2,1)S(1)}, bf16[1,1,1,548]{3,2,1,0:T(2,128)(2,1)S(1)}, u32[]{:S(2)}, u32[]{:S(2)}) collective-permute-start(bf16[1,1,1,548]{3,2,1,0:T(2,128)(2,1)S(1)} %get-tuple-element.72), channel_id=1, source_target_pairs={{0,6},{1,7},{2,8},{3,9},{4,10},{5,11},{6,12},{7,13},{8,14},{9,15},... | collective-permute-start | bytes 3296 | tf_op jit(solution)/shard_map/while/body/eval_jaxpr/ppermute | solution.py:179
  54.5 9.6 %collective-permute-start.6 = (bf16[1,1,1,548]{3,2,1,0:T(2,128)(2,1)S(1)}, bf16[1,1,1,548]{3,2,1,0:T(2,128)(2,1)S(1)}, u32[]{:S(2)}, u32[]{:S(2)}) collective-permute-start(bf16[1,1,1,548]{3,2,1,0:T(2,128)(2,1)S(1)} %get-tuple-element.71), channel_id=1, source_target_pairs={{0,7},{1,8},{2,9},{3,10},{4,11},{5,12},{6,13},{7,14},{8,15},{9,0},... | collective-permute-start | bytes 3296 | tf_op jit(solution)/shard_map/while/body/eval_jaxpr/ppermute | solution.py:179
  56.8 8.0 %collective-permute-start.7 = (bf16[1,1,1,548]{3,2,1,0:T(2,128)(2,1)S(1)}, bf16[1,1,1,548]{3,2,1,0:T(2,128)(2,1)S(1)}, u32[]{:S(2)}, u32[]{:S(2)}) collective-permute-start(bf16[1,1,1,548]{3,2,1,0:T(2,128)(2,1)S(1)} %get-tuple-element.70), channel_id=1, source_target_pairs={{0,8},{1,9},{2,10},{3,11},{4,12},{5,13},{6,14},{7,15},{8,0},{9,1},... | collective-permute-start | bytes 3296 | tf_op jit(solution)/shard_map/while/body/eval_jaxpr/ppermute | solution.py:179
  58.1 7.4 %collective-permute-start.8 = (bf16[1,1,1,548]{3,2,1,0:T(2,128)(2,1)S(1)}, bf16[1,1,1,548]{3,2,1,0:T(2,128)(2,1)S(1)}, u32[]{:S(2)}, u32[]{:S(2)}) collective-permute-start(bf16[1,1,1,548]{3,2,1,0:T(2,128)(2,1)S(1)} %get-tuple-element.69), channel_id=1, source_target_pairs={{0,9},{1,10},{2,11},{3,12},{4,13},{5,14},{6,15},{7,0},{8,1},{9,2},... | collective-permute-start | bytes 3296 | tf_op jit(solution)/shard_map/while/body/eval_jaxpr/ppermute | solution.py:179
  58.1 8.6 %collective-permute-start.9 = (bf16[1,1,1,548]{3,2,1,0:T(2,128)(2,1)S(1)}, bf16[1,1,1,548]{3,2,1,0:T(2,128)(2,1)S(1)}, u32[]{:S(2)}, u32[]{:S(2)}) collective-permute-start(bf16[1,1,1,548]{3,2,1,0:T(2,128)(2,1)S(1)} %get-tuple-element.68), channel_id=1, source_target_pairs={{0,10},{1,11},{2,12},{3,13},{4,14},{5,15},{6,0},{7,1},{8,2},{9,3},... | collective-permute-start | bytes 3296 | tf_op jit(solution)/shard_map/while/body/eval_jaxpr/ppermute | solution.py:179
  60.7 8.2 %collective-permute-start.10 = (bf16[1,1,1,548]{3,2,1,0:T(2,128)(2,1)S(1)}, bf16[1,1,1,548]{3,2,1,0:T(2,128)(2,1)S(1)}, u32[]{:S(2)}, u32[]{:S(2)}) collective-permute-start(bf16[1,1,1,548]{3,2,1,0:T(2,128)(2,1)S(1)} %get-tuple-element.67), channel_id=1, source_target_pairs={{0,11},{1,12},{2,13},{3,14},{4,15},{5,0},{6,1},{7,2},{8,3},{9,4},{... | collective-permute-start | bytes 3296 | tf_op jit(solution)/shard_map/while/body/eval_jaxpr/ppermute | solution.py:179
  64.1 4.9 %collective-permute-start.11 = (bf16[1,1,1,548]{3,2,1,0:T(2,128)(2,1)S(1)}, bf16[1,1,1,548]{3,2,1,0:T(2,128)(2,1)S(1)}, u32[]{:S(2)}, u32[]{:S(2)}) collective-permute-start(bf16[1,1,1,548]{3,2,1,0:T(2,128)(2,1)S(1)} %get-tuple-element.66), channel_id=1, source_target_pairs={{0,12},{1,13},{2,14},{3,15},{4,0},{5,1},{6,2},{7,3},{8,4},{9,5},{1... | collective-permute-start | bytes 3296 | tf_op jit(solution)/shard_map/while/body/eval_jaxpr/ppermute | solution.py:179
  64.8 4.2 %collective-permute-start.12 = (bf16[1,1,1,548]{3,2,1,0:T(2,128)(2,1)S(1)}, bf16[1,1,1,548]{3,2,1,0:T(2,128)(2,1)S(1)}, u32[]{:S(2)}, u32[]{:S(2)}) collective-permute-start(bf16[1,1,1,548]{3,2,1,0:T(2,128)(2,1)S(1)} %get-tuple-element.65), channel_id=1, source_target_pairs={{0,13},{1,14},{2,15},{3,0},{4,1},{5,2},{6,3},{7,4},{8,5},{9,6},{10... | collective-permute-start | bytes 3296 | tf_op jit(solution)/shard_map/while/body/eval_jaxpr/ppermute | solution.py:179
  65.5 3.6 %collective-permute-start.13 = (bf16[1,1,1,548]{3,2,1,0:T(2,128)(2,1)S(1)}, bf16[1,1,1,548]{3,2,1,0:T(2,128)(2,1)S(1)}, u32[]{:S(2)}, u32[]{:S(2)}) collective-permute-start(bf16[1,1,1,548]{3,2,1,0:T(2,128)(2,1)S(1)} %get-tuple-element.64), channel_id=1, source_target_pairs={{0,14},{1,15},{2,0},{3,1},{4,2},{5,3},{6,4},{7,5},{8,6},{9,7},{10,... | collective-permute-start | bytes 3296 | tf_op jit(solution)/shard_map/while/body/eval_jaxpr/ppermute | solution.py:179
  66.7 3.2 %collective-permute-start.14 = (bf16[1,1,1,548]{3,2,1,0:T(2,128)(2,1)S(1)}, bf16[1,1,1,548]{3,2,1,0:T(2,128)(2,1)S(1)}, u32[]{:S(2)}, u32[]{:S(2)}) collective-permute-start(bf16[1,1,1,548]{3,2,1,0:T(2,128)(2,1)S(1)} %get-tuple-element.63), channel_id=1, source_target_pairs={{0,15},{1,0},{2,1},{3,2},{4,3},{5,4},{6,5},{7,6},{8,7},{9,8},{10,9... | collective-permute-start | bytes 3296 | tf_op jit(solution)/shard_map/while/body/eval_jaxpr/ppermute | solution.py:179
